TPU v7x, 256 devices: a whole 4x4x8 slice. The times are simulated.
256 devices in a mesh: grp: 2 (over z_hi), dev: 128 (over x, z_lo, y, core).
Axes of the slice: x: 4, y: 4, z: 8 (z_hi: 2, z_lo: 4; z = z_hi * 4 + z_lo), core: 2. Of those that a mesh axis runs over, the one named last changes fastest.
Arguments:
- voltages: int32 [512, 137216], P('dev', 'grp'), may hold values from -2147483648 to 2147483646
- block_order: int32 [10], replicated, may hold values from 0 to 9, each once
Outputs:
- visibilities: float32 [10, 2, 2, 1024, 128, 128], P('grp', None, None, 'dev')
Inputs may be any that keep to these rules, and one draw needn't show every extreme that they name: `block_order`: a permutation of the block pair numbers.
All inputs are finite; a program needn't handle non-finite values.
Results may differ from a plain program's by a relative error of at most 0.0058.
Values may be sent and summed in bfloat16 or wider, within the bound.
A program may use at most 128 MiB of HBM per device.

v0:
```python
import jax
import jax.numpy as jnp
import numpy as np
from jax import lax
from jax.sharding import PartitionSpec as P

A = 512
FREQ_CHANNELS = 1024
FILTER_TAPS = 4
BLOCK_FRAMES = 64
INTEG_PERIODS = 2
BLOCK = 128


def unpack_packed_words(words):
    pieces = []
    for byte in range(4):
        raw = jnp.bitwise_and(jnp.right_shift(words, 8 * byte), 255)
        pieces.append((raw - 128).astype(jnp.float32) / 64.0)
    return jnp.concatenate(pieces, axis=-1)


def prototype():
    length = 2 * FREQ_CHANNELS
    position = jnp.arange(FILTER_TAPS * length, dtype=jnp.float32) + 0.5
    window = 0.5 - 0.5 * jnp.cos(2.0 * jnp.pi * position / (length * FILTER_TAPS))
    return jnp.sinc(position / length - FILTER_TAPS / 2.0) * window


def dft_table():
    length = 2 * FREQ_CHANNELS
    index = (
        jnp.arange(length, dtype=jnp.int32)[:, None]
        * jnp.arange(FREQ_CHANNELS, dtype=jnp.int32)[None, :]
    )
    angle = 2.0 * jnp.pi / length * (index % length).astype(jnp.float32)
    factor = length ** (-0.5)
    return jnp.stack([jnp.cos(angle) * factor, -jnp.sin(angle) * factor], axis=1).astype(
        jnp.bfloat16
    )


def filter_frames(voltage_samples, coeffs):
    weights = coeffs.reshape(FILTER_TAPS, 2 * FREQ_CHANNELS)
    total = voltage_samples[..., 0:BLOCK_FRAMES, :] * weights[0]
    for shift in range(1, FILTER_TAPS):
        total = total + voltage_samples[..., shift : shift + BLOCK_FRAMES, :] * weights[shift]
    return total.astype(jnp.bfloat16)


def pick(table, index):
    hits = jnp.arange(table.shape[0], dtype=jnp.int32) == index
    return jnp.sum(jnp.where(hits, table, 0)).astype(jnp.int32)


def twist_parts(data):
    width = data.shape[3]
    split = data.reshape(data.shape[:3] + (width // (2 * BLOCK_FRAMES), 2, BLOCK_FRAMES))
    return jnp.stack([split[..., 1, :], -split[..., 0, :]], axis=-2).reshape(data.shape)


def block_gram(data, twisted, slots, block_order, factor):
    upper_rows, upper_cols = np.triu_indices(A // BLOCK)
    pair_rows = jnp.asarray(upper_rows.astype(np.int32))
    pair_cols = jnp.asarray(upper_cols.astype(np.int32))

    def one_slot(slot):
        entry = pick(block_order, slot)
        row = pick(pair_rows, entry) * BLOCK
        col = pick(pair_cols, entry) * BLOCK
        left = lax.dynamic_slice_in_dim(data, row, BLOCK, 2)
        left_twist = lax.dynamic_slice_in_dim(twisted, row, BLOCK, 2)
        right = lax.dynamic_slice_in_dim(data, col, BLOCK, 2)
        real = jnp.einsum("ciak,cibk->icab", left, right, preferred_element_type=jnp.float32)
        imag = jnp.einsum("ciak,cibk->icab", left_twist, right, preferred_element_type=jnp.float32)
        return jnp.stack([real, imag], axis=1) * factor

    return lax.map(one_slot, slots)


def on_device(voltages, block_order):
    antennas_per_device = voltages.shape[0]
    groups = lax.axis_size("grp")
    factor = 1.0 / (groups * BLOCK_FRAMES)
    pair_count = A // BLOCK * (A // BLOCK + 1) // 2
    owned_count = pair_count // groups
    coeffs = prototype()
    table = dft_table()
    voltage_samples = unpack_packed_words(
        voltages.reshape(antennas_per_device, INTEG_PERIODS, -1)
    ).reshape(antennas_per_device, INTEG_PERIODS, BLOCK_FRAMES + FILTER_TAPS - 1, 2 * FREQ_CHANNELS)
    filtered = filter_frames(voltage_samples, coeffs)
    channel_spectra = jnp.einsum(
        "aifn,nrc->ciarf", filtered, table, preferred_element_type=jnp.float32
    )
    channel_spectra = channel_spectra.astype(jnp.bfloat16).reshape(
        FREQ_CHANNELS, INTEG_PERIODS, antennas_per_device, 2 * BLOCK_FRAMES
    )
    data = lax.all_to_all(channel_spectra, "dev", split_axis=0, concat_axis=2, tiled=True)
    twisted = twist_parts(data)
    owned = lax.axis_index("grp") * owned_count + jnp.arange(owned_count, dtype=jnp.int32)
    return block_gram(
        lax.all_gather(data, "grp", axis=3, tiled=True),
        lax.all_gather(twisted, "grp", axis=3, tiled=True),
        owned,
        block_order,
        factor,
    )


def solution(mesh):
    in_specs = (P("dev", "grp"), P())
    out_specs = P("grp", None, None, "dev", None, None)
    return jax.shard_map(
        on_device, mesh=mesh, in_specs=in_specs, out_specs=out_specs, check_vma=False
    )
```

profile of v0, /device:TPU:1, one launch (start us, length us, event | category | flops | bytes accessed | tf_op | source)
XLA Modules:
  0.0 431.1 jit_solution(8316655637687082720)
XLA Ops:
  6.7 35.2 %multiply_convert_fusion = (bf16[2048,1,1024]{2,0,1:T(8,128)(2,1)}, bf16[2048,1,1024]{2,0,1:T(8,128)(2,1)}) fusion(), kind=kLoop, calls=%fused_computation.27 | loop fusion | flops 39845888 | bytes 8388608 | tf_op jit(solution)/shard_map/convert.1
  41.9 2.7 convert_multiply_fusion.3
  46.9 2.4 reshape.173
  49.2 3.4 reshape.175
  52.7 10.2 %pad_maximum_fusion = f32[4,2,137216]{2,1,0:T(2,128)} fusion(f32[4,2,34304]{2,1,0:T(2,128)} %reshape.175, f32[4,2,34304]{2,1,0:T(2,128)S(1)} %reshape.173, f32[4,2,34304]{2,1,0:T(2,128)S(1)} %reshape.171, f32[4,2,34304]{2,1,0:T(2,128)S(1)} %reshape.169), kind=kLoop, calls=%fused_computation.32 | loop fusion | flops 3293184 | bytes 8781824 | tf_op jit(solution)/shard_map/concatenate | solution.py:20
  62.8 6.9 %reshape.164 = f32[4,2,67,2048]{3,2,1,0:T(8,128)} reshape(f32[4,2,137216]{2,1,0:T(2,128)} %pad_maximum_fusion) | data formatting | bytes 8781824 | tf_op jit(solution)/shard_map/reshape | solution.py:91
  69.7 14.4 %convert_bitcast_fusion = bf16[1024,2,4,2,64]{0,4,1,2,3:T(8,128)(2,1)S(1)} fusion(f32[2048]{0:T(1024)S(1)} %get-tuple-element.110, f32[4,2,67,2048]{3,2,1,0:T(8,128)} %reshape.164, f32[2048]{0:T(1024)S(1)} %get-tuple-element.111, f32[2048]{0:T(1024)S(1)} %get-tuple-element.112, f32[2048]{0:T(1024)S(1)} %get-tuple-element.109, ...), kind=kOutput, calls=%fused_computation.45 | convolution fusion | flops 4321181696 | bytes 27295744 | tf_op jit(solution)/shard_map/aifn,nrc->ciarf/dot_general | solution.py:93
  84.3 2.7 copy.21
  87.0 65.7 %all_to_all.18 = bf16[1024,2,4,128]{3,2,1,0:T(4,128)(2,1)S(1)} all-to-all(bf16[1024,2,4,128]{3,2,1,0:T(4,128)(2,1)} %copy.21), channel_id=1, replica_groups=mesh['grp'=2,'dev'=128] {'dev'}, dimensions={0} | all-to-all | bytes 4194304 | tf_op jit(solution)/shard_map/all_to_all | solution.py:99
  153.0 1.7 copy.23
  154.7 8.4 %reshape.166 = bf16[8,2,512,1,2,64]{5,4,0,2,1,3:T(2,128)(2,1)} reshape(bf16[8,2,128,4,128]{4,0,3,2,1:T(8,128)(2,1)} %copy.23) | data formatting | bytes 4194304 | tf_op jit(solution)/shard_map/reshape | solution.py:58
  163.2 9.6 %fusion.43 = (bf16[8,2,512,1,1,64]{5,4,0,2,1,3:T(2,128)(2,1)S(1)}, bf16[8,2,512,1,1,64]{5,4,0,2,1,3:T(2,128)(2,1)S(1)}) fusion(bf16[8,2,512,1,2,64]{5,4,0,2,1,3:T(2,128)(2,1)} %reshape.166), kind=kLoop, calls=%fused_computation.79 | loop fusion | flops 524288 | bytes 4194304 | tf_op jit(solution)/shard_map/slice | solution.py:59
  172.8 12.0 %pad_maximum_fusion.1 = bf16[8,2,512,1,2,64]{5,4,0,2,1,3:T(2,128)(2,1)} fusion(bf16[8,2,512,1,1,64]{5,4,0,2,1,3:T(2,128)(2,1)S(1)} %get-tuple-element.104, bf16[8,2,512,1,1,64]{5,4,0,2,1,3:T(2,128)(2,1)S(1)} %get-tuple-element.103), kind=kLoop, calls=%fused_computation.42 | loop fusion | flops 4194304 | bytes 4194304 | tf_op jit(solution)/shard_map/stack | solution.py:59
  184.9 10.6 %copy.25 = bf16[8,2,512,1,2,64]{2,5,4,1,0,3:T(8,128)(2,1)} copy(bf16[8,2,512,1,2,64]{5,4,0,2,1,3:T(2,128)(2,1)} %pad_maximum_fusion.1) | data formatting | bytes 4194304 | tf_op jit(solution)/shard_map/stack | solution.py:59
  195.5 68.0 %all-gather.3.cloned.1.call-done = bf16[8,2,512,256]{3,0,2,1:T(8,128)(2,1)} async-done(((bf16[8,2,512,128]{3,0,2,1:T(8,128)(2,1)}), bf16[8,2,512,256]{3,0,2,1:T(8,128)(2,1)}) %all-gather.3.cloned.1.call-update) | async-done | bytes 4194320 | tf_op jit(solution)/shard_map/all_gather | solution.py:103
  263.5 5.1 %copy.26 = bf16[8,2,512,256]{3,2,0,1:T(8,128)(2,1)} copy(bf16[8,2,512,256]{3,0,2,1:T(8,128)(2,1)} %all-gather.3.cloned.1.call-done) | data formatting | bytes 8388608
  268.6 104.8 %all-gather.5.cloned.1.call-done = bf16[8,2,512,256]{2,3,1,0:T(8,128)(2,1)} async-done(((bf16[8,2,512,128]{2,3,1,0:T(8,128)(2,1)}), bf16[8,2,512,256]{2,3,1,0:T(8,128)(2,1)}) %all-gather.5.cloned.1.call-update) | async-done | bytes 4194320 | tf_op jit(solution)/shard_map/all_gather | solution.py:104
  373.4 50.9 %while.11 = (s32[]{:T(128)}, f32[5,2,2,8,128,128]{5,4,3,2,1,0:T(8,128)}, s32[5]{0:T(128)S(1)}, s32[10]{0:T(128)S(1)}, bf16[8,2,512,256]{3,2,0,1:T(8,128)(2,1)}, ...) while((s32[]{:T(128)}, ...), condition=%wide.region_4.5_spmd.clone, body=%wide.region_0.4_spmd.sunk.clone.sunk | while | flops 269484096 | bytes 10486649 | solution.py:78
  378.0 2.0 convolution_bitcast_fusion.5
  380.0 2.0 convolution_bitcast_fusion.4
  382.1 1.5 copy_dynamic-update-slice_fusion.2
  388.2 2.1 convolution_bitcast_fusion.5
  390.3 2.0 convolution_bitcast_fusion.4
  392.3 1.5 copy_dynamic-update-slice_fusion.2
  398.4 2.0 convolution_bitcast_fusion.5
  400.4 2.0 convolution_bitcast_fusion.4
  402.5 1.5 copy_dynamic-update-slice_fusion.2
  408.6 2.0 convolution_bitcast_fusion.5
  410.6 2.0 convolution_bitcast_fusion.4
  412.6 1.5 copy_dynamic-update-slice_fusion.2
  418.8 2.0 convolution_bitcast_fusion.5
  420.8 2.0 convolution_bitcast_fusion.4
  (36 shorter events, 21.0 us)
Async XLA Ops:
  6.5 256.9 %all-gather.3.cloned.1.call-start = ((), (), s32[]{:S(2)}) async-start(), calls=%async_computation.1 | async-start | bytes 6291456 | tf_op jit(solution)/shard_map/all_gather | solution.py:103
  6.7 35.2 %copy-start = (s32[4,68608]{1,0:T(4,128)S(1)}, s32[4,68608]{1,0:T(4,128)}, u32[]{:S(2)}) copy-start(s32[4,68608]{1,0:T(4,128)} %param.6) | copy-start | bytes 3293188
  154.7 218.7 %all-gather.5.cloned.1.call-start = ((), (), s32[]{:S(2)}) async-start(), calls=%async_computation.2 | async-start | bytes 6291456 | tf_op jit(solution)/shard_map/all_gather | solution.py:104
  195.5 177.9 %copy-start.1 = (s32[10]{0:T(128)S(1)}, s32[10]{0:T(128)}, u32[]{:S(2)}) copy-start(s32[10]{0:T(128)} %constant.119.clone..sunk.2) | copy-start | bytes 124
  195.5 177.9 %copy-start.2 = (s32[10]{0:T(128)S(1)}, s32[10]{0:T(128)}, u32[]{:S(2)}) copy-start(s32[10]{0:T(128)} %constant.120.clone..sunk.2) | copy-start | bytes 124
  195.5 177.9 %copy-start.3 = (s32[10]{0:T(128)S(1)}, s32[10]{0:T(128)}, u32[]{:S(2)}) copy-start(s32[10]{0:T(128)} %param.7) | copy-start | bytes 124
Sparse Core Ops, SparseCore 0:
  154.8 108.6 all-gather.2
  265.3 108.0 all-gather.4
where the time goes:
time: 432 us; the launch traced here: 431 us
  waiting for transfers between devices  173 us (40%)
  other arithmetic  90.8 us (21%)
  blocking collectives  65.7 us (15%)
  local copies, waits for them, and re-layouts  46.9 us (11%)
  matrix products  34.7 us (8%)
  between operations  13.5 us (3%)
  loops' own time  6.67 us (2%)
    all_gather x1, waiting for transfers between devices, on_device(): lax.all_gather(twisted, 'grp', axis=3, tiled=True)  105 us
    all_gather x1, waiting for transfers between devices, on_device(): lax.all_gather(data, 'grp', axis=3, tiled=True)  68 us
    all_to_all x1, blocking collectives, on_device(): lax.all_to_all(channel_spectra, 'dev', split_axis=0, concat_axis=2, tiled...  65.7 us
    another operation x1, other arithmetic  35.2 us
    dot_general x1, matrix products, on_device(): jnp.einsum('aifn,nrc->ciarf', filtered, table, preferred_element_type=jnp...  14.4 us
    reduce_sum x10, other arithmetic, pick(): return jnp.sum(jnp.where(hits, table, 0)).astype(jnp.int32)  13.5 us
    another operation x1, other arithmetic, twist_parts(): jnp.stack([split[..., 1, :], -split[..., 0, :]], axis=-2)  12 us
    another operation x1, local copies, waits for them, and re-layouts, twist_parts(): jnp.stack([split[..., 1, :], -split[..., 0, :]], axis=-2)  10.6 us
  transfers between devices with their start and end apart: 2, of which 2 were waited for; matrix products, arithmetic and copies ran while one was open for 11% of the time, Pallas kernels for 0%

commit v1 on v0

--- a/solution.py
+++ b/solution.py
@@ -100,7 +100,7 @@
     twisted = twist_parts(data)
     owned = lax.axis_index("grp") * owned_count + jnp.arange(owned_count, dtype=jnp.int32)
     return block_gram(
-        lax.all_gather(data, "grp", axis=3, tiled=True),
+        jnp.concatenate(lax.all_gather(data, "grp"), axis=3),
         lax.all_gather(twisted, "grp", axis=3, tiled=True),
         owned,
         block_order,

time: 432 us -> 433 us (level)
    all_gather x0 -> x2, local copies, waits for them, and re-layouts: none -> 8.24 us  [on_device(): lax.all_gather(data, 'grp')]
    all_gather x1, waiting for transfers between devices: 105 us -> 97 us  [on_device(): lax.all_gather(twisted, 'grp', axis=3, tiled=True)]
    all_gather x1, waiting for transfers between devices: 68 us -> 73 us  [on_device(): lax.all_gather(data, 'grp')]
    reshape x1, local copies, waits for them, and re-layouts: 8.43 us -> 3.48 us  [twist_parts(): data.reshape(data.shape[:3] + (width // (2 * BLOCK_FRAMES), 2, BLOCK_FRAM...]
where the time goes in v1:
time: 433 us; the launch traced here: 432 us
  waiting for transfers between devices  170 us (39%)
  other arithmetic  90.8 us (21%)
  blocking collectives  65.7 us (15%)
  local copies, waits for them, and re-layouts  50.3 us (12%)
  matrix products  34.7 us (8%)
  between operations  13.5 us (3%)
  loops' own time  6.67 us (2%)
    all_gather x1, waiting for transfers between devices, on_device(): lax.all_gather(twisted, 'grp', axis=3, tiled=True)  97 us
    all_gather x1, waiting for transfers between devices, on_device(): lax.all_gather(data, 'grp')  73 us
    all_to_all x1, blocking collectives, on_device(): lax.all_to_all(channel_spectra, 'dev', split_axis=0, concat_axis=2, tiled...  65.7 us
    another operation x1, other arithmetic  35.2 us
    dot_general x1, matrix products, on_device(): jnp.einsum('aifn,nrc->ciarf', filtered, table, preferred_element_type=jnp...  14.4 us
    reduce_sum x10, other arithmetic, pick(): return jnp.sum(jnp.where(hits, table, 0)).astype(jnp.int32)  13.5 us
    another operation x1, other arithmetic, twist_parts(): jnp.stack([split[..., 1, :], -split[..., 0, :]], axis=-2)  12 us
    another operation x1, local copies, waits for them, and re-layouts, twist_parts(): jnp.stack([split[..., 1, :], -split[..., 0, :]], axis=-2)  10.6 us
  transfers between devices with their start and end apart: 2, of which 2 were waited for; matrix products, arithmetic and copies ran while one was open for 11% of the time, Pallas kernels for 0%

profile of v1, /device:TPU:1, one launch (start us, length us, event | category | flops | bytes accessed | tf_op | source)
XLA Modules:
  0.0 431.6 jit_solution(15584859130727086265)
XLA Ops:
  6.7 35.2 %multiply_convert_fusion = (bf16[2048,1,1024]{2,0,1:T(8,128)(2,1)}, bf16[2048,1,1024]{2,0,1:T(8,128)(2,1)}) fusion(), kind=kLoop, calls=%fused_computation.27 | loop fusion | flops 39845888 | bytes 8388608 | tf_op jit(solution)/shard_map/convert.1
  41.9 2.7 convert_multiply_fusion.3
  46.9 2.4 reshape.182
  49.2 3.4 reshape.184
  52.7 10.2 %pad_maximum_fusion = f32[4,2,137216]{2,1,0:T(2,128)} fusion(f32[4,2,34304]{2,1,0:T(2,128)} %reshape.184, f32[4,2,34304]{2,1,0:T(2,128)S(1)} %reshape.182, f32[4,2,34304]{2,1,0:T(2,128)S(1)} %reshape.180, f32[4,2,34304]{2,1,0:T(2,128)S(1)} %reshape.178), kind=kLoop, calls=%fused_computation.32 | loop fusion | flops 3293184 | bytes 8781824 | tf_op jit(solution)/shard_map/concatenate | solution.py:20
  62.8 6.9 %reshape.171 = f32[4,2,67,2048]{3,2,1,0:T(8,128)} reshape(f32[4,2,137216]{2,1,0:T(2,128)} %pad_maximum_fusion) | data formatting | bytes 8781824 | tf_op jit(solution)/shard_map/reshape | solution.py:91
  69.7 14.4 %convert_bitcast_fusion = bf16[1024,2,4,2,64]{0,4,1,2,3:T(8,128)(2,1)S(1)} fusion(f32[2048]{0:T(1024)S(1)} %get-tuple-element.110, f32[4,2,67,2048]{3,2,1,0:T(8,128)} %reshape.171, f32[2048]{0:T(1024)S(1)} %get-tuple-element.111, f32[2048]{0:T(1024)S(1)} %get-tuple-element.112, f32[2048]{0:T(1024)S(1)} %get-tuple-element.109, ...), kind=kOutput, calls=%fused_computation.45 | convolution fusion | flops 4321181696 | bytes 27295744 | tf_op jit(solution)/shard_map/aifn,nrc->ciarf/dot_general | solution.py:93
  84.3 2.7 copy.23
  87.0 65.7 %all_to_all.15 = bf16[1024,2,4,128]{3,2,1,0:T(4,128)(2,1)S(1)} all-to-all(bf16[1024,2,4,128]{3,2,1,0:T(4,128)(2,1)} %copy.23), channel_id=1, replica_groups=mesh['grp'=2,'dev'=128] {'dev'}, dimensions={0} | all-to-all | bytes 4194304 | tf_op jit(solution)/shard_map/all_to_all | solution.py:99
  153.4 1.8 copy.26
  155.2 3.5 reshape.175
  158.7 9.6 %fusion.43 = (bf16[8,2,512,1,1,64]{5,4,0,2,1,3:T(2,128)(2,1)S(1)}, bf16[8,2,512,1,1,64]{5,4,0,2,1,3:T(2,128)(2,1)S(1)}) fusion(bf16[8,2,512,1,2,64]{5,4,0,2,1,3:T(2,128)(2,1)} %reshape.175), kind=kLoop, calls=%fused_computation.79 | loop fusion | flops 524288 | bytes 4194304 | tf_op jit(solution)/shard_map/slice | solution.py:59
  168.3 12.0 %pad_maximum_fusion.1 = bf16[8,2,512,1,2,64]{5,4,0,2,1,3:T(2,128)(2,1)} fusion(bf16[8,2,512,1,1,64]{5,4,0,2,1,3:T(2,128)(2,1)S(1)} %get-tuple-element.104, bf16[8,2,512,1,1,64]{5,4,0,2,1,3:T(2,128)(2,1)S(1)} %get-tuple-element.103), kind=kLoop, calls=%fused_computation.42 | loop fusion | flops 4194304 | bytes 4194304 | tf_op jit(solution)/shard_map/stack | solution.py:59
  180.4 10.6 %copy.29 = bf16[8,2,512,1,2,64]{2,5,4,1,0,3:T(8,128)(2,1)} copy(bf16[8,2,512,1,2,64]{5,4,0,2,1,3:T(2,128)(2,1)} %pad_maximum_fusion.1) | data formatting | bytes 4194304 | tf_op jit(solution)/shard_map/stack | solution.py:59
  191.0 73.0 %all-gather.3.cloned.1.call-done = bf16[2,8,2,512,128]{4,3,2,1,0:T(8,128)(2,1)} async-done(((bf16[1,8,2,512,128]{4,3,2,1,0:T(8,128)(2,1)}), bf16[2,8,2,512,128]{4,3,2,1,0:T(8,128)(2,1)}) %all-gather.3.cloned.1.call-update) | async-done | bytes 4194320 | tf_op jit(solution)/shard_map/all_gather | solution.py:103
  264.0 6.5 %copy.27 = bf16[2,8,2,512,128]{3,4,0,2,1:T(8,128)(2,1)} copy(bf16[2,8,2,512,128]{4,3,2,1,0:T(8,128)(2,1)} %all-gather.3.cloned.1.call-done) | data formatting | bytes 8388608 | tf_op jit(solution)/shard_map/all_gather | solution.py:103
  270.4 6.5 %copy.30 = bf16[8,2,512,256]{3,2,0,1:T(8,128)(2,1)} copy(bf16[8,2,512,256]{2,3,1,0:T(8,128)(2,1)} %bitcast.41) | data formatting | bytes 8388608
  276.9 97.0 %all-gather.5.cloned.1.call-done = bf16[8,2,512,256]{2,3,1,0:T(8,128)(2,1)} async-done(((bf16[8,2,512,128]{2,3,1,0:T(8,128)(2,1)}), bf16[8,2,512,256]{2,3,1,0:T(8,128)(2,1)}) %all-gather.5.cloned.1.call-update) | async-done | bytes 4194320 | tf_op jit(solution)/shard_map/all_gather | solution.py:104
  373.9 50.9 %while.11 = (s32[]{:T(128)}, f32[5,2,2,8,128,128]{5,4,3,2,1,0:T(8,128)}, s32[5]{0:T(128)S(1)}, s32[10]{0:T(128)S(1)}, bf16[8,2,512,256]{3,2,0,1:T(8,128)(2,1)}, ...) while((s32[]{:T(128)}, ...), condition=%wide.region_4.5_spmd.clone, body=%wide.region_0.4_spmd.sunk.clone.sunk | while | flops 269484096 | bytes 10486649 | solution.py:78
  378.5 2.0 convolution_bitcast_fusion.5
  380.5 2.0 convolution_bitcast_fusion.4
  382.6 1.5 copy_dynamic-update-slice_fusion.2
  388.7 2.1 convolution_bitcast_fusion.5
  390.8 2.0 convolution_bitcast_fusion.4
  392.8 1.5 copy_dynamic-update-slice_fusion.2
  399.0 2.0 convolution_bitcast_fusion.5
  400.9 2.0 convolution_bitcast_fusion.4
  409.1 2.0 convolution_bitcast_fusion.5
  411.1 2.0 convolution_bitcast_fusion.4
  413.2 1.5 copy_dynamic-update-slice_fusion.2
  419.3 2.0 convolution_bitcast_fusion.5
  421.3 2.0 convolution_bitcast_fusion.4
  (38 shorter events, 22.9 us)
Async XLA Ops:
  6.5 257.4 %all-gather.3.cloned.1.call-start = ((), (), s32[]{:S(2)}) async-start(), calls=%async_computation.1 | async-start | bytes 6291456 | tf_op jit(solution)/shard_map/all_gather | solution.py:103
  6.7 35.2 %copy-start = (s32[4,68608]{1,0:T(4,128)S(1)}, s32[4,68608]{1,0:T(4,128)}, u32[]{:S(2)}) copy-start(s32[4,68608]{1,0:T(4,128)} %param.6) | copy-start | bytes 3293188
  155.2 218.7 %all-gather.5.cloned.1.call-start = ((), (), s32[]{:S(2)}) async-start(), calls=%async_computation.2 | async-start | bytes 6291456 | tf_op jit(solution)/shard_map/all_gather | solution.py:104
  270.4 103.5 %copy-start.1 = (s32[10]{0:T(128)S(1)}, s32[10]{0:T(128)}, u32[]{:S(2)}) copy-start(s32[10]{0:T(128)} %constant.119.clone..sunk.2) | copy-start | bytes 124
  270.4 103.5 %copy-start.2 = (s32[10]{0:T(128)S(1)}, s32[10]{0:T(128)}, u32[]{:S(2)}) copy-start(s32[10]{0:T(128)} %constant.120.clone..sunk.2) | copy-start | bytes 124
  270.4 103.5 %copy-start.3 = (s32[10]{0:T(128)S(1)}, s32[10]{0:T(128)}, u32[]{:S(2)}) copy-start(s32[10]{0:T(128)} %param.7) | copy-start | bytes 124
Sparse Core Ops, SparseCore 0:
  155.3 108.6 all-gather.2
  265.8 108.0 all-gather.4
